TPU v7x, 256 devices: a whole 4x4x8 slice. The times are simulated.
256 devices in a mesh: dp: 16 (over y, x), rows: 16 (over z, core).
Axes of the slice: x: 4, y: 4, z: 8, core: 2. Of those that a mesh axis runs over, the one named last changes fastest.
Arguments:
- grad_out: bfloat16 [8192, 4096], P('dp', 'rows'), may hold values from -0.375 to 0.375
- activations: bfloat16 [8192, 4096], P('dp', 'rows'), may hold values from -6 to 6
- error_feedback: float32 [16, 4096, 4096], P('dp', 'rows'), may hold values from -6 to 6
- momentum: bfloat16 [4096, 4096], P('rows'), may hold values from -1.1953125 to 1.1953125
- right_factor: float32 [4096, 128], P('rows'), may hold values from -0.09375 to 0.09375
Outputs:
- new_error: float32 [16, 4096, 4096], P('dp', 'rows')
- new_momentum: bfloat16 [4096, 4096], P('rows')
- new_right: float32 [4096, 128], P('rows')
All inputs are finite; a program needn't handle non-finite values.
Results may differ from a plain program's by a relative error of at most 0.0012.
Values may be sent and summed in bfloat16 or wider, within the bound.
A program may use at most 64 MiB of HBM per device.

v0:
```python
import jax
import jax.numpy as jnp
from jax import lax
from jax.sharding import PartitionSpec as P

PASSES = 2
MOMENTUM_RATE = 0.9
HIGHEST = lax.Precision.HIGHEST


def from_everyone(value, axis):
    copies = jnp.broadcast_to(value, (lax.axis_size(axis), *value.shape))
    return lax.all_to_all(copies, axis, split_axis=0, concat_axis=0, tiled=True)


def joined_along(tiles, dim):
    lengths = list(tiles.shape[1:])
    lengths[dim] *= tiles.shape[0]
    return jnp.moveaxis(tiles, 0, dim).reshape(lengths)


def gathered_copies(value, axis, dim):
    tiles = from_everyone(value, axis)
    return joined_along(tiles, dim)


def of_everyone(value, axis):
    everything = from_everyone(value, axis)
    return jnp.sum(everything, axis=0)


def total_of_pieces(value, axis):
    return lax.all_gather(value, axis).sum(0)


def cut_along(value, dim, count):
    lengths = value.shape
    tiles = value.reshape(*lengths[:dim], count, lengths[dim] // count, *lengths[dim + 1 :])
    return jnp.moveaxis(tiles, dim, 0)


def sent_and_summed(value, axis, dim):
    count = lax.axis_size(axis)
    tiles = lax.all_to_all(cut_along(value, dim, count), axis, 0, 0, tiled=True)
    return jnp.sum(tiles, axis=0)


def per_device(grad_out, activations, error_feedback, momentum, right_factor):
    replicas = lax.axis_size("dp")
    grad_local = lax.dot_general(
        grad_out,
        lax.all_gather(activations, "rows", axis=1, tiled=True),
        (((0,), (0,)), ((), ())),
        preferred_element_type=jnp.float32,
    )
    merged = grad_local + error_feedback[0]
    right_full = gathered_copies(right_factor, "rows", 0)
    left_factor = None
    own_rows = None
    for pass_index in range(PASSES):
        local_term = jnp.dot(
            merged, right_full, precision=HIGHEST, preferred_element_type=jnp.float32
        )
        left_factor = of_everyone(local_term, "dp") / replicas
        gram_local = jnp.dot(
            left_factor.T, left_factor, precision=HIGHEST, preferred_element_type=jnp.float32
        )
        gram_matrix = total_of_pieces(gram_local, "rows")
        cholesky_lower = jnp.linalg.cholesky(gram_matrix)
        left_factor = jax.scipy.linalg.solve_triangular(cholesky_lower, left_factor.T, lower=True).T
        right_term = lax.dot_general(
            merged,
            left_factor,
            (((0,), (0,)), ((), ())),
            precision=HIGHEST,
            preferred_element_type=jnp.float32,
        )
        own_rows = sent_and_summed(right_term, "rows", 0)
        own_rows = of_everyone(own_rows, "dp") / replicas
        right_full = gathered_copies(own_rows, "rows", 0)
    approx = jnp.dot(
        left_factor, right_full.T, precision=HIGHEST, preferred_element_type=jnp.float32
    )
    new_error = (merged - approx)[None]
    new_momentum = (MOMENTUM_RATE * momentum.astype(jnp.float32) + approx).astype(jnp.bfloat16)
    return (new_error, new_momentum, own_rows)


def solution(mesh):
    return jax.shard_map(
        per_device,
        mesh=mesh,
        in_specs=(
            P("dp", "rows"),
            P("dp", "rows"),
            P("dp", "rows", None),
            P("rows", None),
            P("rows", None),
        ),
        out_specs=(P("dp", "rows", None), P("rows", None), P("rows", None)),
        check_vma=False,
    )
```

profile of v0, /device:TPU:1, one launch (start us, length us, event | category | flops | bytes accessed | tf_op | source)
XLA Modules:
  0.0 616.3 jit_solution(16566047498738973250)
XLA Ops:
  7.9 2.4 broadcast_in_dim.25
  10.3 10.0 %all-to-all-start = ((f32[16,256,128]{2,1,0:T(8,128)}), f32[16,256,128]{2,1,0:T(8,128)S(1)}, u32[]{:S(2)}, u32[]{:S(2)}) async-start(f32[16,256,128]{2,1,0:T(8,128)} %broadcast_in_dim.25), calls=%async_computation | async-start | bytes 4194304 | tf_op jit(solution)/shard_map/all_to_all | solution.py:13
  20.4 75.3 %all-gather.6.cloned.1.call-done = bf16[512,4096]{1,0:T(8,128)(2,1)} async-done(((bf16[512,256]{1,0:T(8,128)(2,1)}), bf16[512,4096]{1,0:T(8,128)(2,1)}) %all-gather.6.cloned.1.call-update) | async-done | bytes 4194320 | tf_op jit(solution)/shard_map/all_gather | solution.py:52
  95.7 6.8 %convolution_add_fusion = f32[256,4096]{1,0:T(8,128)} fusion(bf16[512,256]{1,0:T(8,128)(2,1)S(1)} %copy-done, bf16[512,4096]{1,0:T(8,128)(2,1)} %all-gather.6.cloned.1.call-done, f32[1,256,4096]{2,1,0:T(8,128)} %param.10), kind=kOutput, calls=%fused_computation | convolution fusion | flops 1074790400 | bytes 12845056 | tf_op jit(solution)/shard_map/dot_general | solution.py:50
  102.5 5.9 fusion.26
  108.6 34.5 %all_to_all.45 = f32[16,256,128]{2,1,0:T(8,128)S(1)} all-to-all(f32[16,256,128]{2,1,0:T(8,128)S(1)} %broadcast_in_dim.26), channel_id=1, replica_groups=mesh['dp'=16,'rows'=16] {'dp'}, dimensions={0} | all-to-all | bytes 4194304 | tf_op jit(solution)/shard_map/all_to_all | solution.py:13
  144.4 34.3 %all-gather.8.cloned.1.call-done = f32[2048,128]{1,0:T(8,128)} async-done(((f32[128,128]{1,0:T(8,128)}), f32[2048,128]{1,0:T(8,128)}) %all-gather.8.cloned.1.call-update) | async-done | bytes 1048592 | tf_op jit(solution)/shard_map/all_gather | solution.py:33
  178.7 1.3 reduce_sum.73
  180.1 11.7 %cholesky.44 = f32[128,128]{1,0:T(8,128)S(1)} custom-call(f32[128,128]{1,0:T(8,128)S(1)} %fusion.15), custom_call_target="Cholesky" | custom-call | tf_op jit(solution)/shard_map/jit(cholesky)/cholesky | solution.py:69
  193.2 9.8 %custom-call.6 = f32[1,128,128]{1,2,0:T(8,128)S(1)} custom-call(f32[1,128,128]{2,1,0:T(8,128)S(1)} %fusion.10), custom_call_target="InvertDiagBlocksLowerTriangular" | custom-call | tf_op jit(solution)/shard_map/jit(_solve_triangular)/triangular_solve | solution.py:70
  203.3 8.7 %fusion.27 = f32[4096,128]{1,0:T(8,128)S(1)} fusion(f32[256,4096]{1,0:T(8,128)} %convolution_add_fusion, f32[128,256]{1,0:T(8,128)S(1)} %fusion.2), kind=kOutput, calls=%fused_computation.41 | convolution fusion | flops 1610612736 | bytes 6422528 | tf_op jit(solution)/shard_map/dot_general | solution.py:71
  212.0 55.3 %all_to_all.46 = f32[16,256,128]{2,1,0:T(8,128)S(1)} all-to-all(f32[16,256,128]{2,1,0:T(8,128)S(1)} %bitcast.49), channel_id=1, replica_groups=mesh['dp'=16,'rows'=16] {'rows'}, dimensions={0} | all-to-all | bytes 4194304 | tf_op jit(solution)/shard_map/all_to_all | solution.py:44
  267.6 34.7 %all_to_all.47 = f32[16,256,128]{2,1,0:T(8,128)S(1)} all-to-all(f32[16,256,128]{2,1,0:T(8,128)S(1)} %broadcast_in_dim.27), channel_id=1, replica_groups=mesh['dp'=16,'rows'=16] {'dp'}, dimensions={0} | all-to-all | bytes 4194304 | tf_op jit(solution)/shard_map/all_to_all | solution.py:13
  302.6 54.5 %all_to_all.48 = f32[16,256,128]{2,1,0:T(8,128)S(1)} all-to-all(f32[16,256,128]{2,1,0:T(8,128)S(1)} %broadcast_in_dim.28), channel_id=1, replica_groups=mesh['dp'=16,'rows'=16] {'rows'}, dimensions={0} | all-to-all | bytes 4194304 | tf_op jit(solution)/shard_map/all_to_all | solution.py:13
  357.1 3.5 fusion.28
  360.8 31.1 %all_to_all.49 = f32[16,256,128]{2,1,0:T(8,128)S(1)} all-to-all(f32[16,256,128]{2,1,0:T(8,128)S(1)} %broadcast_in_dim.29), channel_id=1, replica_groups=mesh['dp'=16,'rows'=16] {'dp'}, dimensions={0} | all-to-all | bytes 4194304 | tf_op jit(solution)/shard_map/all_to_all | solution.py:13
  393.0 32.6 %all-gather.10.cloned.1.call-done = f32[2048,128]{1,0:T(8,128)} async-done(((f32[128,128]{1,0:T(8,128)}), f32[2048,128]{1,0:T(8,128)}) %all-gather.10.cloned.1.call-update) | async-done | bytes 1048592 | tf_op jit(solution)/shard_map/all_gather | solution.py:33
  427.0 11.7 %cholesky.55 = f32[128,128]{1,0:T(8,128)S(1)} custom-call(f32[128,128]{1,0:T(8,128)S(1)} %fusion.13), custom_call_target="Cholesky" | custom-call | tf_op jit(solution)/shard_map/jit(cholesky)/cholesky | solution.py:69
  440.1 9.8 %custom-call.7 = f32[1,128,128]{1,2,0:T(8,128)S(1)} custom-call(f32[1,128,128]{2,1,0:T(8,128)S(1)} %fusion.11), custom_call_target="InvertDiagBlocksLowerTriangular" | custom-call | tf_op jit(solution)/shard_map/jit(_solve_triangular)/triangular_solve | solution.py:70
  450.2 8.7 %fusion.29 = f32[4096,128]{1,0:T(8,128)S(1)} fusion(f32[256,4096]{1,0:T(8,128)} %convolution_add_fusion, f32[128,256]{1,0:T(8,128)S(1)} %fusion), kind=kOutput, calls=%fused_computation.43 | convolution fusion | flops 1610612736 | bytes 6422528 | tf_op jit(solution)/shard_map/dot_general | solution.py:71
  458.8 55.3 %all_to_all.50 = f32[16,256,128]{2,1,0:T(8,128)S(1)} all-to-all(f32[16,256,128]{2,1,0:T(8,128)S(1)} %bitcast.51), channel_id=1, replica_groups=mesh['dp'=16,'rows'=16] {'rows'}, dimensions={0} | all-to-all | bytes 4194304 | tf_op jit(solution)/shard_map/all_to_all | solution.py:44
  514.4 34.7 %all_to_all.51 = f32[16,256,128]{2,1,0:T(8,128)S(1)} all-to-all(f32[16,256,128]{2,1,0:T(8,128)S(1)} %broadcast_in_dim.30), channel_id=1, replica_groups=mesh['dp'=16,'rows'=16] {'dp'}, dimensions={0} | all-to-all | bytes 4194304 | tf_op jit(solution)/shard_map/all_to_all | solution.py:13
  549.5 54.5 %all_to_all.52 = f32[16,256,128]{2,1,0:T(8,128)S(1)} all-to-all(f32[16,256,128]{2,1,0:T(8,128)S(1)} %broadcast_in_dim.31), channel_id=1, replica_groups=mesh['dp'=16,'rows'=16] {'rows'}, dimensions={0} | all-to-all | bytes 4194304 | tf_op jit(solution)/shard_map/all_to_all | solution.py:13
  604.0 5.8 add_convert_fusion
  (46 shorter events, 9.7 us)
Async XLA Ops:
  7.2 88.5 %copy-start = (bf16[512,256]{1,0:T(8,128)(2,1)S(1)}, bf16[512,256]{1,0:T(8,128)(2,1)}, u32[]{:S(2)}) copy-start(bf16[512,256]{1,0:T(8,128)(2,1)} %param.8) | copy-start | bytes 786436
  7.2 88.5 %all-gather.6.cloned.1.call-start = ((), (), s32[]{:S(2)}) async-start(), calls=%async_computation.9 | async-start | bytes 4456448 | tf_op jit(solution)/shard_map/all_gather | solution.py:52
  10.3 92.1 %all-to-all-start = ((f32[16,256,128]{2,1,0:T(8,128)}), f32[16,256,128]{2,1,0:T(8,128)S(1)}, u32[]{:S(2)}, u32[]{:S(2)}) async-start(f32[16,256,128]{2,1,0:T(8,128)} %broadcast_in_dim.25), calls=%async_computation | async-start | bytes 4194304 | tf_op jit(solution)/shard_map/all_to_all | solution.py:13
  20.3 158.4 %all-gather.8.cloned.1.call-start = ((), (), s32[]{:S(2)}) async-start(), calls=%async_computation.10 | async-start | bytes 1114112 | tf_op jit(solution)/shard_map/all_gather | solution.py:33
  144.2 281.4 %all-gather.10.cloned.1.call-start = ((), (), s32[]{:S(2)}) async-start(), calls=%async_computation.11 | async-start | bytes 1114112 | tf_op jit(solution)/shard_map/all_gather | solution.py:33
  302.6 54.6 %copy-start.1 = (f32[256,4096]{1,0:T(8,128)S(1)}, f32[256,4096]{1,0:T(8,128)}, u32[]{:S(2)}) copy-start(f32[256,4096]{1,0:T(8,128)} %convolution_add_fusion) | copy-start | bytes 12582916
  549.2 54.8 %copy-start.4 = (f32[256,128]{1,0:T(8,128)}, f32[256,128]{1,0:T(8,128)S(1)}, u32[]{:S(2)}) copy-start(f32[256,128]{1,0:T(8,128)S(1)} %broadcast_multiply_fusion) | copy-start | bytes 393220
  549.2 54.8 %copy-start.3 = (bf16[256,4096]{1,0:T(8,128)(2,1)S(1)}, bf16[256,4096]{1,0:T(8,128)(2,1)}, u32[]{:S(2)}) copy-start(bf16[256,4096]{1,0:T(8,128)(2,1)} %param.11) | copy-start | bytes 6291460
  549.5 54.6 %copy-start.2 = (f32[256,4096]{1,0:T(8,128)S(1)}, f32[256,4096]{1,0:T(8,128)}, u32[]{:S(2)}) copy-start(f32[256,4096]{1,0:T(8,128)} %convolution_add_fusion) | copy-start | bytes 12582916
Sparse Core Ops, SparseCore 0:
  9.7 85.8 all-gather.5
  144.3 34.3 all-gather.7
  393.1 32.4 all-gather.9
where the time goes:
time: 617 us; the launch traced here: 616 us
  blocking collectives  355 us (58%)
  waiting for transfers between devices  143 us (23%)
  other arithmetic  49 us (8%)
  matrix products  41.9 us (7%)
  between operations  14 us (2%)
  starting transfers between devices  10.3 us (2%)
    all_to_all x6, blocking collectives, from_everyone(): return lax.all_to_all(copies, axis, split_axis=0, concat_axis=0, tiled=True)  244 us
    all_to_all x2, blocking collectives, sent_and_summed(): tiles = lax.all_to_all(cut_along(value, dim, count), axis, 0, 0, tiled=True)  111 us
    all_gather x1, waiting for transfers between devices, per_device(): lax.all_gather(activations, 'rows', axis=1, tiled=True)  75.3 us
    all_gather x2, waiting for transfers between devices, total_of_pieces(): return lax.all_gather(value, axis).sum(0)  66.9 us
    another operation x6, other arithmetic, per_device(): cholesky_lower = jnp.linalg.cholesky(gram_matrix)  24.8 us
    another operation x4, other arithmetic, per_device(): jax.scipy.linalg.solve_triangular(cholesky_lower, left_factor.T, lower=True)  20.9 us
    dot_general x2, matrix products, per_device(): lax.dot_general(merged, left_factor, (((0,), (0,)), ((), ())), precision=...  17.3 us
  transfers between devices with their start and end apart: 4, of which 3 were waited for; matrix products, arithmetic and copies ran while one was open for 1% of the time, Pallas kernels for 0%

commit v1 on v0

--- a/solution.py
+++ b/solution.py
@@ -6,6 +6,18 @@
 PASSES = 2
 MOMENTUM_RATE = 0.9
 HIGHEST = lax.Precision.HIGHEST
+
+
+def doubled_up(shard, axis, dim):
+    ways, here = (lax.axis_size(axis), lax.axis_index(axis))
+    grown, reach = (shard, 1)
+    while reach < ways:
+        theirs = lax.ppermute(grown, axis, [(d, d ^ reach) for d in range(ways)])
+        mine_first = jnp.concatenate([grown, theirs], axis=dim)
+        theirs_first = jnp.concatenate([theirs, grown], axis=dim)
+        grown = jnp.where(here & reach == 0, mine_first, theirs_first)
+        reach = 2 * reach
+    return grown
 
 
 def from_everyone(value, axis):
@@ -49,7 +61,7 @@
     replicas = lax.axis_size("dp")
     grad_local = lax.dot_general(
         grad_out,
-        lax.all_gather(activations, "rows", axis=1, tiled=True),
+        doubled_up(activations, "rows", 1),
         (((0,), (0,)), ((), ())),
         preferred_element_type=jnp.float32,
     )

time: 617 us -> 757 us (1.23); the launches traced: 616 us -> 748 us
  waiting for transfers between devices: 143 us -> 243 us
  local copies, waits for them, and re-layouts: 3.81 us -> 19.8 us
  other arithmetic: 49 us -> 60.1 us
  starting transfers between devices: 10.3 us -> 18.7 us
    ppermute x0 -> x4, waiting for transfers between devices: none -> 142 us  [doubled_up(): theirs = lax.ppermute(grown, axis, [(d, d ^ reach) for d in range(ways)])]
    all_gather x1 -> x0, waiting for transfers between devices: 75.3 us -> none  [per_device(): lax.all_gather(activations, 'rows', axis=1, tiled=True)]
    all_to_all x1, waiting for transfers between devices: 0.01 us -> 22.6 us  [from_everyone(): return lax.all_to_all(copies, axis, split_axis=0, concat_axis=0, tiled=True)]
    all_gather x2, waiting for transfers between devices: 66.9 us -> 78.5 us  [total_of_pieces(): return lax.all_gather(value, axis).sum(0)]
    unnamed x10 -> x14, local copies, waits for them, and re-layouts: 0.03 us -> 11.3 us
    ppermute x0 -> x4, starting transfers between devices: none -> 10.3 us  [doubled_up(): theirs = lax.ppermute(grown, axis, [(d, d ^ reach) for d in range(ways)])]
  transfers between devices with their start and end apart: 4 -> 7, of which waited for: 3 -> 7; matrix products, arithmetic and copies ran while one was open for 1% -> 3% of each run, Pallas kernels for 0% -> 0%
where the time goes in v1:
time: 757 us; the launch traced here: 748 us
  blocking collectives  349 us (46%)
  waiting for transfers between devices  243 us (32%)
  other arithmetic  60.1 us (8%)
  matrix products  43.1 us (6%)
  local copies, waits for them, and re-layouts  19.8 us (3%)
  starting transfers between devices  18.7 us (2%)
  between operations  14.6 us (2%)
    all_to_all x6, blocking collectives, from_everyone(): return lax.all_to_all(copies, axis, split_axis=0, concat_axis=0, tiled=True)  238 us
    ppermute x4, waiting for transfers between devices, doubled_up(): theirs = lax.ppermute(grown, axis, [(d, d ^ reach) for d in range(ways)])  142 us
    all_to_all x2, blocking collectives, sent_and_summed(): tiles = lax.all_to_all(cut_along(value, dim, count), axis, 0, 0, tiled=True)  111 us
    all_gather x2, waiting for transfers between devices, total_of_pieces(): return lax.all_gather(value, axis).sum(0)  78.5 us
    another operation x6, other arithmetic, per_device(): cholesky_lower = jnp.linalg.cholesky(gram_matrix)  24.8 us
    all_to_all x1, waiting for transfers between devices, from_everyone(): return lax.all_to_all(copies, axis, split_axis=0, concat_axis=0, tiled=True)  22.6 us
    another operation x4, other arithmetic, per_device(): jax.scipy.linalg.solve_triangular(cholesky_lower, left_factor.T, lower=True)  20.9 us
    dot_general x2, matrix products, per_device(): jnp.dot(merged, right_full, precision=HIGHEST, preferred_element_type=jnp...  15.3 us
  transfers between devices with their start and end apart: 7, of which 7 were waited for; matrix products, arithmetic and copies ran while one was open for 3% of the time, Pallas kernels for 0%

profile of v1, /device:TPU:1, one launch (start us, length us, event | category | flops | bytes accessed | tf_op | source)
XLA Modules:
  0.0 748.1 jit_solution(10704423115440872313)
XLA Ops:
  13.1 13.1 %collective-permute-done.1 = bf16[512,512]{1,0:T(8,128)(2,1)S(1)} collective-permute-done((bf16[512,512]{1,0:T(8,128)(2,1)S(1)}, bf16[512,512]{1,0:T(8,128)(2,1)S(1)}, u32[]{:S(2)}, u32[]{:S(2)}) %collective-permute-start.1) | collective-permute-done | bytes 524320 | tf_op jit(solution)/shard_map/ppermute | solution.py:15
  29.8 7.8 %all-to-all-start = ((f32[16,256,128]{2,1,0:T(8,128)}), f32[16,256,128]{2,1,0:T(8,128)S(1)}, u32[]{:S(2)}, u32[]{:S(2)}) async-start(f32[16,256,128]{2,1,0:T(8,128)} %broadcast_in_dim.25), calls=%async_computation | async-start | bytes 4194304 | tf_op jit(solution)/shard_map/all_to_all | solution.py:25
  37.7 65.3 %collective-permute-done.2 = bf16[512,1024]{1,0:T(8,128)(2,1)} collective-permute-done((bf16[512,1024]{1,0:T(8,128)(2,1)S(1)}, bf16[512,1024]{1,0:T(8,128)(2,1)}, u32[]{:S(2)}, u32[]{:S(2)}) %collective-permute-start.2) | collective-permute-done | bytes 1048608 | tf_op jit(solution)/shard_map/ppermute | solution.py:15
  117.4 62.1 %collective-permute-done.3 = bf16[512,2048]{1,0:T(8,128)(2,1)} collective-permute-done((bf16[512,2048]{1,0:T(8,128)(2,1)}, bf16[512,2048]{1,0:T(8,128)(2,1)}, u32[]{:S(2)}, u32[]{:S(2)}) %collective-permute-start.3) | collective-permute-done | bytes 2097184 | tf_op jit(solution)/shard_map/ppermute | solution.py:15
  179.6 8.8 %fusion = f32[256,4096]{0,1:T(8,128)} fusion(bf16[512,256]{1,0:T(8,128)(2,1)S(1)} %copy-done, bf16[512,2048]{1,0:T(8,128)(2,1)} %collective-permute-done.3, bf16[512,2048]{1,0:T(8,128)(2,1)} %maximum_select_fusion.2, f32[1,256,4096]{1,2,0:T(8,128)} %copy.18, pred[]{:T(512)S(6)} %eq.12), kind=kOutput, calls=%fused_computation.1 | convolution fusion | flops 1093664768 | bytes 12845057 | tf_op jit(solution)/shard_map/dot_general | solution.py:62
  188.4 22.6 %all-to-all-done = f32[16,256,128]{2,1,0:T(8,128)S(1)} async-done(((f32[16,256,128]{2,1,0:T(8,128)}), f32[16,256,128]{2,1,0:T(8,128)S(1)}, u32[]{:S(2)}, u32[]{:S(2)}) %all-to-all-start) | async-done | bytes 2097184 | tf_op jit(solution)/shard_map/all_to_all | solution.py:25
  211.0 8.5 %fusion.34 = f32[256,128]{1,0:T(8,128)S(1)} fusion(f32[256,4096]{0,1:T(8,128)} %fusion, f32[4096,128]{1,0:T(8,128)S(1)} %bitcast.50), kind=kOutput, calls=%fused_computation.52 | convolution fusion | flops 1610612736 | bytes 6422528 | tf_op jit(solution)/shard_map/dot_general | solution.py:73
  219.7 28.3 %all_to_all.45 = f32[16,256,128]{2,1,0:T(8,128)S(1)} all-to-all(f32[16,256,128]{2,1,0:T(8,128)S(1)} %broadcast_in_dim.26), channel_id=1, replica_groups=mesh['dp'=16,'rows'=16] {'dp'}, dimensions={0} | all-to-all | bytes 4194304 | tf_op jit(solution)/shard_map/all_to_all | solution.py:25
  249.8 45.9 %all-gather.5.cloned.1.call-done = f32[2048,128]{1,0:T(8,128)} async-done(((f32[128,128]{1,0:T(8,128)}), f32[2048,128]{1,0:T(8,128)}) %all-gather.5.cloned.1.call-update) | async-done | bytes 1048592 | tf_op jit(solution)/shard_map/all_gather | solution.py:45
  297.1 11.7 %cholesky.44 = f32[128,128]{1,0:T(8,128)S(1)} custom-call(f32[128,128]{1,0:T(8,128)S(1)} %fusion.22), custom_call_target="Cholesky" | custom-call | tf_op jit(solution)/shard_map/jit(cholesky)/cholesky | solution.py:81
  310.1 9.8 %custom-call.6 = f32[1,128,128]{1,2,0:T(8,128)S(1)} custom-call(f32[1,128,128]{2,1,0:T(8,128)S(1)} %fusion.17), custom_call_target="InvertDiagBlocksLowerTriangular" | custom-call | tf_op jit(solution)/shard_map/jit(_solve_triangular)/triangular_solve | solution.py:82
  325.6 55.3 %all_to_all.46 = f32[16,256,128]{2,1,0:T(8,128)S(1)} all-to-all(f32[16,256,128]{2,1,0:T(8,128)S(1)} %bitcast.51), channel_id=1, replica_groups=mesh['dp'=16,'rows'=16] {'rows'}, dimensions={0} | all-to-all | bytes 4194304 | tf_op jit(solution)/shard_map/all_to_all | solution.py:56
  381.1 34.7 %all_to_all.47 = f32[16,256,128]{2,1,0:T(8,128)S(1)} all-to-all(f32[16,256,128]{2,1,0:T(8,128)S(1)} %broadcast_in_dim.27), channel_id=1, replica_groups=mesh['dp'=16,'rows'=16] {'dp'}, dimensions={0} | all-to-all | bytes 4194304 | tf_op jit(solution)/shard_map/all_to_all | solution.py:25
  416.2 54.7 %all_to_all.48 = f32[16,256,128]{2,1,0:T(8,128)S(1)} all-to-all(f32[16,256,128]{2,1,0:T(8,128)S(1)} %broadcast_in_dim.28), channel_id=1, replica_groups=mesh['dp'=16,'rows'=16] {'rows'}, dimensions={0} | all-to-all | bytes 4194304 | tf_op jit(solution)/shard_map/all_to_all | solution.py:25
  470.9 6.8 fusion.36
  477.9 31.2 %all_to_all.49 = f32[16,256,128]{2,1,0:T(8,128)S(1)} all-to-all(f32[16,256,128]{2,1,0:T(8,128)S(1)} %broadcast_in_dim.29), channel_id=1, replica_groups=mesh['dp'=16,'rows'=16] {'dp'}, dimensions={0} | all-to-all | bytes 4194304 | tf_op jit(solution)/shard_map/all_to_all | solution.py:25
  510.3 32.6 %all-gather.7.cloned.1.call-done = f32[2048,128]{1,0:T(8,128)} async-done(((f32[128,128]{1,0:T(8,128)}), f32[2048,128]{1,0:T(8,128)}) %all-gather.7.cloned.1.call-update) | async-done | bytes 1048592 | tf_op jit(solution)/shard_map/all_gather | solution.py:45
  544.3 11.7 %cholesky.55 = f32[128,128]{1,0:T(8,128)S(1)} custom-call(f32[128,128]{1,0:T(8,128)S(1)} %fusion.20), custom_call_target="Cholesky" | custom-call | tf_op jit(solution)/shard_map/jit(cholesky)/cholesky | solution.py:81
  557.4 9.8 %custom-call.7 = f32[1,128,128]{1,2,0:T(8,128)S(1)} custom-call(f32[1,128,128]{2,1,0:T(8,128)S(1)} %fusion.18), custom_call_target="InvertDiagBlocksLowerTriangular" | custom-call | tf_op jit(solution)/shard_map/jit(_solve_triangular)/triangular_solve | solution.py:82
  572.8 55.3 %all_to_all.50 = f32[16,256,128]{2,1,0:T(8,128)S(1)} all-to-all(f32[16,256,128]{2,1,0:T(8,128)S(1)} %bitcast.53), channel_id=1, replica_groups=mesh['dp'=16,'rows'=16] {'rows'}, dimensions={0} | all-to-all | bytes 4194304 | tf_op jit(solution)/shard_map/all_to_all | solution.py:56
  628.4 34.7 %all_to_all.51 = f32[16,256,128]{2,1,0:T(8,128)S(1)} all-to-all(f32[16,256,128]{2,1,0:T(8,128)S(1)} %broadcast_in_dim.30), channel_id=1, replica_groups=mesh['dp'=16,'rows'=16] {'dp'}, dimensions={0} | all-to-all | bytes 4194304 | tf_op jit(solution)/shard_map/all_to_all | solution.py:25
  663.4 54.6 %all_to_all.52 = f32[16,256,128]{2,1,0:T(8,128)S(1)} all-to-all(f32[16,256,128]{2,1,0:T(8,128)S(1)} %broadcast_in_dim.31), channel_id=1, replica_groups=mesh['dp'=16,'rows'=16] {'rows'}, dimensions={0} | all-to-all | bytes 4194304 | tf_op jit(solution)/shard_map/all_to_all | solution.py:25
  718.1 5.7 add_convert_fusion
  729.4 6.0 subtract_bitcast_fusion
  (60 shorter events, 56.4 us)
Async XLA Ops:
  7.2 172.4 %copy-start = (bf16[512,256]{1,0:T(8,128)(2,1)S(1)}, bf16[512,256]{1,0:T(8,128)(2,1)}, u32[]{:S(2)}) copy-start(bf16[512,256]{1,0:T(8,128)(2,1)} %param.8) | copy-start | bytes 786436
  7.2 21.1 %copy-start.5 = (f32[256,128]{1,0:T(8,128)S(1)}, f32[256,128]{1,0:T(8,128)}, u32[]{:S(2)}) copy-start(f32[256,128]{1,0:T(8,128)} %param.12) | copy-start | bytes 393220
  7.2 4.7 collective-permute-start
  13.0 13.2 %collective-permute-start.1 = (bf16[512,512]{1,0:T(8,128)(2,1)S(1)}, bf16[512,512]{1,0:T(8,128)(2,1)S(1)}, u32[]{:S(2)}, u32[]{:S(2)}) collective-permute-start(bf16[512,512]{1,0:T(8,128)(2,1)S(1)} %maximum_select_fusion.4), channel_id=1, source_target_pairs={{0,2},{1,3},{2,0},{3,1},{4,6},{5,7},{6,4},{7,5},{8,10},{9,11},{10,... | collective-permute-start | bytes 1572872 | tf_op jit(solution)/shard_map/ppermute | solution.py:15
  26.5 76.5 %collective-permute-start.2 = (bf16[512,1024]{1,0:T(8,128)(2,1)S(1)}, bf16[512,1024]{1,0:T(8,128)(2,1)}, u32[]{:S(2)}, u32[]{:S(2)}) collective-permute-start(bf16[512,1024]{1,0:T(8,128)(2,1)S(1)} %maximum_select_fusion.3), channel_id=1, source_target_pairs={{0,4},{1,5},{2,6},{3,7},{4,0},{5,1},{6,2},{7,3},{8,12},{9,13},{10,... | collective-permute-start | bytes 3145736 | tf_op jit(solution)/shard_map/ppermute | solution.py:15
  29.8 181.2 %all-to-all-start = ((f32[16,256,128]{2,1,0:T(8,128)}), f32[16,256,128]{2,1,0:T(8,128)S(1)}, u32[]{:S(2)}, u32[]{:S(2)}) async-start(f32[16,256,128]{2,1,0:T(8,128)} %broadcast_in_dim.25), calls=%async_computation | async-start | bytes 4194304 | tf_op jit(solution)/shard_map/all_to_all | solution.py:25
  37.6 258.0 %all-gather.5.cloned.1.call-start = ((), (), s32[]{:S(2)}) async-start(), calls=%async_computation.9 | async-start | bytes 1114112 | tf_op jit(solution)/shard_map/all_gather | solution.py:45
  106.6 72.9 %collective-permute-start.3 = (bf16[512,2048]{1,0:T(8,128)(2,1)}, bf16[512,2048]{1,0:T(8,128)(2,1)}, u32[]{:S(2)}, u32[]{:S(2)}) collective-permute-start(bf16[512,2048]{1,0:T(8,128)(2,1)} %maximum_select_fusion.2), channel_id=1, source_target_pairs={{0,8},{1,9},{2,10},{3,11},{4,12},{5,13},{6,14},{7,15},{8,0},{9,1},... | collective-permute-start | bytes 6291464 | tf_op jit(solution)/shard_map/ppermute | solution.py:15
  249.2 293.7 %all-gather.7.cloned.1.call-start = ((), (), s32[]{:S(2)}) async-start(), calls=%async_computation.10 | async-start | bytes 1114112 | tf_op jit(solution)/shard_map/all_gather | solution.py:45
  416.1 54.7 %copy-start.2 = (f32[256,4096]{0,1:T(8,128)S(1)}, f32[256,4096]{0,1:T(8,128)}, u32[]{:S(2)}) copy-start(f32[256,4096]{0,1:T(8,128)} %fusion) | copy-start | bytes 12582916
  663.2 54.9 %copy-start.4 = (f32[256,128]{1,0:T(8,128)}, f32[256,128]{1,0:T(8,128)S(1)}, u32[]{:S(2)}) copy-start(f32[256,128]{1,0:T(8,128)S(1)} %broadcast_multiply_fusion) | copy-start | bytes 393220
  663.4 54.7 %copy-start.3 = (bf16[256,4096]{1,0:T(8,128)(2,1)S(1)}, bf16[256,4096]{1,0:T(8,128)(2,1)}, u32[]{:S(2)}) copy-start(bf16[256,4096]{1,0:T(8,128)(2,1)} %param.11) | copy-start | bytes 6291460
  735.3 5.6 copy-start.1
Sparse Core Ops, SparseCore 0:
  249.3 46.2 all-gather.4
  510.4 32.4 all-gather.6
